TPU v7x, 128 devices: a whole 4x4x4 slice. The times are simulated.
128 devices in a mesh: row: 16 (over y, x), col: 8 (over z, core).
Axes of the slice: x: 4, y: 4, z: 4, core: 2. Of those that a mesh axis runs over, the one named last changes fastest.
Arguments:
- moments: float32 [2, 128, 128, 6144], P(None, None, 'row', 'col'), may hold values from -6 to 6
- owner_counts: int32 [16], replicated, may hold values from 1 to 16, 128 in all
Outputs:
- normalized: float32 [2, 32768, 6144], P(None, 'row', 'col')
- scales: float32 [2, 256], P(None, 'row')
- energy: float32 [2, 256], P(None, 'row')
Inputs may be any that keep to these rules, and one draw needn't show every extreme that they name: owner_counts sums to 128, and its largest entry is exactly 16.
All inputs are finite; a program needn't handle non-finite values.
Results may differ from a plain program's by a relative error of at most 0.00002.
Values sent between devices are 32-bit elements.
A program may use at most 128 MiB of HBM per device.

v0:
```python
import functools
import jax
import jax.numpy as jnp
from jax import lax
from jax.sharding import PartitionSpec as P
from jax.experimental import pallas as pl
from jax.experimental.pallas import tpu as pltpu

SIDE = 4
GROUPS = SIDE * SIDE
HALF = 8
TIERS = (17, 18, 19, 20, 21, 22, 23, 24, 26, 28, 32)
MESH = pl.DeviceIdType.MESH
TURNS = (1, 3, 2)


def plan_kernel(count_ref, plan_ref, tier_ref):
    groups = SIDE * SIDE
    n = [count_ref[g] for g in range(groups)]
    low = [jnp.maximum(v - HALF, 0) for v in n]
    high = [jnp.minimum(v, HALF) for v in n]
    a = [(n[g] + (g // SIDE + g % SIDE) % 2) // 2 for g in range(groups)]
    col = [sum(a[x::SIDE]) for x in range(SIDE)]
    row = [sum(n[y * SIDE:(y + 1) * SIDE]) - sum(a[y * SIDE:(y + 1) * SIDE]) for y in range(SIDE)]
    for _ in range(2):
        for g in range(groups):
            y, x = divmod(g, SIDE)
            new = jnp.clip(a[g] - ((col[x] - row[y] + 1) >> 1), low[g], high[g])
            col[x] = col[x] + new - a[g]
            row[y] = row[y] + a[g] - new
            a[g] = new
    need = functools.reduce(jnp.maximum, col + row)
    tier = jnp.int32(0)
    for limit in TIERS[:-1]:
        tier = tier + (need > limit).astype(jnp.int32)
    tier_ref[0] = tier
    start = jnp.int32(0)
    at_x, at_y = [jnp.int32(0)] * SIDE, [jnp.int32(0)] * SIDE
    for g in range(groups):
        y, x = divmod(g, SIDE)
        plan_ref[g] = a[g]
        plan_ref[groups + g] = start
        plan_ref[2 * groups + g] = at_x[x]
        plan_ref[3 * groups + g] = at_y[y]
        plan_ref[4 * groups + g] = n[g]
        start = start + n[g]
        at_x[x] = at_x[x] + a[g]
        at_y[y] = at_y[y] + n[g] - a[g]


def move_kernel(
    slots, cols, plan_in, moments_ref, x2_ref, y2_ref, stats_ref,
    mom0, mom1, send_x, send_y, got_x0, got_x1, got_y0, got_y1, out_x, out_y,
    pieces, stat_a, stat_b, stat_c, all_a, all_b, all_c,
    plan_ref, plan_sem, load_sem, send1, recv1, send2, recv2, sa, ra, sb, rb,
):
    mom = (mom0, mom1)
    got_x = (got_x0, got_x1)
    got_y = (got_y0, got_y1)
    tensors = 2
    me = lax.axis_index("row")
    c = lax.axis_index("col")
    y, x = me // SIDE, me % SIDE
    blocks = mom0.shape[0]

    loads = [
        pltpu.make_async_copy(moments_ref.at[t], mom[t], load_sem.at[t])
        for t in range(tensors)
    ]
    table = pltpu.make_async_copy(plan_in, plan_ref, plan_sem)
    table.start()
    for load in loads:
        load.start()

    def x_peer(d):
        return {"row": y * SIDE + (x + d) % SIDE}

    def y_peer(d):
        return {"row": ((y + d) % SIDE) * SIDE + x}

    barrier = pltpu.get_barrier_semaphore()
    for d in TURNS:
        pl.semaphore_signal(barrier, inc=1, device_id=x_peer(d), device_id_type=MESH)
        pl.semaphore_signal(barrier, inc=1, device_id=y_peer(d), device_id_type=MESH)
    for d in range(1, cols):
        pl.semaphore_signal(barrier, inc=1, device_id={"col": (c + d) % cols}, device_id_type=MESH)

    def order_x(xd):
        at = [plan_ref[2 * GROUPS + i * SIDE + xd] for i in range(SIDE)]
        base = [plan_ref[GROUPS + i * SIDE + xd] - at[i] for i in range(SIDE)]

        def block_of(k):
            b = base[0]
            for i in range(1, SIDE):
                b = jnp.where(k >= at[i], base[i], b)
            return jnp.clip(b + k, 0, blocks - 1)

        return block_of

    def order_y(yd):
        at = [plan_ref[3 * GROUPS + yd * SIDE + i] for i in range(SIDE)]
        base = [
            plan_ref[GROUPS + yd * SIDE + i] + plan_ref[yd * SIDE + i] - at[i]
            for i in range(SIDE)
        ]

        def block_of(k):
            b = base[0]
            for i in range(1, SIDE):
                b = jnp.where(k >= at[i], base[i], b)
            return jnp.clip(b + k, 0, blocks - 1)

        return block_of

    def pack1(t, block_of, dst):
        def step(k, carry):
            dst[k] = mom[t][block_of(k)]
            return carry

        lax.fori_loop(0, slots, step, 0, unroll=2)

    table.wait()
    pl.semaphore_wait(barrier, 2 * (SIDE - 1) + cols - 1)

    first = [[], []]
    for t in range(tensors):
        loads[t].wait()
        for i, d in enumerate(TURNS):
            pack1(t, order_x((x + d) % SIDE), send_x.at[t, i])
            copy = pltpu.make_async_remote_copy(
                send_x.at[t, i], got_x[t].at[x], send1.at[t, 0, i], recv1.at[t, 0, i],
                device_id=x_peer(d), device_id_type=MESH)
            copy.start()
            first[t].append(copy)
            pack1(t, order_y((y + d) % SIDE), send_y.at[t, i])
            copy = pltpu.make_async_remote_copy(
                send_y.at[t, i], got_y[t].at[y], send1.at[t, 1, i], recv1.at[t, 1, i],
                device_id=y_peer(d), device_id_type=MESH)
            copy.start()
            first[t].append(copy)
        pack1(t, order_x(x), got_x[t].at[x])
        pack1(t, order_y(y), got_y[t].at[y])

    width = mom0.shape[2]
    for t in range(tensors):
        def measure(k, carry, t=t):
            rows = pl.ds(pl.multiple_of(k * 8, 8), 8)
            peak = None
            for w in range(0, width, 128):
                v = mom[t][rows, :, w:w + 128]
                m, q = jnp.abs(v), v * v
                peak, total = (m, q) if peak is None else (jnp.maximum(peak, m), total + q)
            pieces[t, rows, :] = jnp.max(peak, axis=1)
            pieces[2 + t, rows, :] = jnp.sum(total, axis=1)
            return carry

        lax.fori_loop(0, blocks // 8, measure, 0)
    stat_a[...] = jnp.zeros_like(stat_a)
    for t in range(tensors):
        stat_a[t:t + 1, :] = jnp.max(pieces[t].T, axis=0, keepdims=True)
        stat_a[2 + t:3 + t, :] = jnp.sum(pieces[2 + t].T, axis=0, keepdims=True)
    is_peak = lax.broadcasted_iota(jnp.int32, stat_a.shape, 0) < tensors

    def join(mine, others, n):
        v = mine[...]
        for i in range(n):
            o = others[i]
            v = jnp.where(is_peak, jnp.maximum(v, o), v + o)
        return v

    stage = []
    for d in range(1, cols):
        copy = pltpu.make_async_remote_copy(
            stat_a, all_a.at[d - 1], sa.at[d - 1], ra.at[d - 1],
            device_id={"col": (c + d) % cols}, device_id_type=MESH)
        copy.start()
        stage.append(copy)
    for copy in stage:
        copy.wait()
    stat_b[...] = join(stat_a, all_a, cols - 1)
    stage = []
    for i, d in enumerate(TURNS):
        copy = pltpu.make_async_remote_copy(
            stat_b, all_b.at[i], sb.at[0, i], rb.at[0, i],
            device_id=x_peer(d), device_id_type=MESH)
        copy.start()
        stage.append(copy)

    def pack2(got, offset, dst):
        def step(j, carry):
            k = jnp.minimum(offset + j, slots - 1)
            for s in range(SIDE):
                dst[j, s] = got[s, k]
            return carry

        lax.fori_loop(0, HALF, step, 0)

    second = []
    for t in range(tensors):
        for copy in first[t]:
            copy.wait_recv()
        if t == 1:
            for copy in stage:
                copy.wait()
            stat_c[...] = join(stat_b, all_b, SIDE - 1)
            stage = []
            for i, d in enumerate(TURNS):
                copy = pltpu.make_async_remote_copy(
                    stat_c, all_c.at[i], sb.at[1, i], rb.at[1, i],
                    device_id=y_peer(d), device_id_type=MESH)
                copy.start()
                stage.append(copy)
        for i, d in enumerate(TURNS):
            yd, xd = (y + d) % SIDE, (x + d) % SIDE
            pack2(got_x[t], plan_ref[2 * GROUPS + yd * SIDE + x], out_x.at[t, i])
            copy = pltpu.make_async_remote_copy(
                out_x.at[t, i], x2_ref.at[y, t], send2.at[t, 0, i], recv2.at[t, 0, i],
                device_id=y_peer(d), device_id_type=MESH)
            copy.start()
            second.append(copy)
            pack2(got_y[t], plan_ref[3 * GROUPS + y * SIDE + xd], out_y.at[t, i])
            copy = pltpu.make_async_remote_copy(
                out_y.at[t, i], y2_ref.at[x, t], send2.at[t, 1, i], recv2.at[t, 1, i],
                device_id=x_peer(d), device_id_type=MESH)
            copy.start()
            second.append(copy)
        pack2(got_x[t], plan_ref[2 * GROUPS + me], x2_ref.at[y, t])
        pack2(got_y[t], plan_ref[3 * GROUPS + me], y2_ref.at[x, t])

    for t in range(tensors):
        for copy in first[t]:
            copy.wait_send()
    for copy in stage:
        copy.wait()
    stats_ref[...] = join(stat_c, all_c, SIDE - 1)
    for copy in second:
        copy.wait()


def place_kernel(
    full_size, plan_ref, stats_ref, x2_ref, y2_ref, norm_ref, scale_out, energy_out,
    outb, zeros, inverse, scale_ref, energy_ref, out_sem, small_sem,
):
    tensors, capacity = scale_ref.shape
    me = lax.axis_index("row")
    a, start, n = plan_ref[me], plan_ref[GROUPS + me], plan_ref[4 * GROUPS + me]
    zeros[...] = jnp.zeros_like(zeros)
    rows = zeros.shape[0]

    def put(t, j, src):
        at = pl.ds(pl.multiple_of(j * rows, rows), rows)
        return pltpu.make_async_copy(src, norm_ref.at[t, at], out_sem.at[t, j])

    for t in range(tensors):
        lax.fori_loop(n, capacity, lambda j, _: (put(t, j, zeros).start(), _)[1], 0)

    lanes = stats_ref.shape[1]
    mine = pltpu.roll(stats_ref[...], lax.rem(lanes - start, lanes), 1)
    lane = lax.broadcasted_iota(jnp.int32, mine.shape, 1)
    scale = jnp.where(lane < n, jnp.maximum(mine, 1.0), 1.0)
    energy = jnp.where(lane < n, mine / full_size, 0.0)
    scale_ref[...] = scale[:tensors, :capacity]
    energy_ref[...] = energy[tensors:2 * tensors, :capacity]
    inv = 1.0 / scale
    pick = lax.broadcasted_iota(jnp.int32, (capacity, lanes), 0)
    pick = pick == lax.broadcasted_iota(jnp.int32, (capacity, lanes), 1)
    for t in range(tensors):
        own = jnp.where(pick, jnp.broadcast_to(inv[t:t + 1], pick.shape), 0.0)
        inverse[t] = jnp.broadcast_to(jnp.sum(own, axis=1, keepdims=True), pick.shape)
    small = [
        pltpu.make_async_copy(scale_ref, scale_out, small_sem.at[0]),
        pltpu.make_async_copy(energy_ref, energy_out, small_sem.at[1]),
    ]
    for copy in small:
        copy.start()

    for t in range(tensors):
        def scaled(j, carry, t=t, swap=False):
            factor = jnp.broadcast_to(inverse[t, pl.ds(j, 1), :], (8, lanes))
            for p in range(SIDE):
                for q in range(SIDE):
                    r = (q * SIDE + p) if swap else (p * SIDE + q)
                    for w in range(0, outb.shape[3], lanes):
                        at = slice(w, w + lanes)
                        part = y2_ref[p, t, j - a, q, :, at] if swap else x2_ref[p, t, j, q, :, at]
                        outb[t, j, r * 8:r * 8 + 8, at] = part * factor
            put(t, j, outb.at[t, j]).start()
            return carry

        lax.fori_loop(0, a, functools.partial(scaled, swap=False), 0)
        lax.fori_loop(a, n, functools.partial(scaled, swap=True), 0)
    for t in range(tensors):
        lax.fori_loop(0, capacity, lambda j, _: (put(t, j, zeros).wait(), _)[1], 0)
    for copy in small:
        copy.wait()


def on_device(moments, owner_counts):
    tensors, blocks, sub, width = moments.shape
    groups, cols = lax.axis_size("row"), lax.axis_size("col")
    capacity = 2 * HALF
    f32, i32 = jnp.float32, jnp.int32
    smem = pl.BlockSpec(memory_space=pltpu.SMEM)
    hbm = pl.BlockSpec(memory_space=pl.ANY)
    vmem = pl.BlockSpec(memory_space=pltpu.VMEM)

    plan, tier = pl.pallas_call(
        plan_kernel,
        out_shape=(jax.ShapeDtypeStruct((128,), i32), jax.ShapeDtypeStruct((1,), i32)),
        in_specs=[smem],
        out_specs=(smem, smem),
        name="plan",
    )(owner_counts)

    def branch(number, slots):
        arrived = pltpu.VMEM((SIDE, tensors, HALF, SIDE, sub, width), f32)
        got = pltpu.VMEM((SIDE, slots, sub, width), f32)
        sent = pltpu.VMEM((tensors, SIDE - 1, slots, sub, width), f32)
        out = pltpu.VMEM((tensors, SIDE - 1, HALF, SIDE, sub, width), f32)
        stat = pltpu.VMEM((8, blocks), f32)
        dma = pltpu.SemaphoreType.DMA
        peers = max(cols - 1, 1)
        piece = 4 * sub * width
        limit = piece * (2 * blocks + 28 * slots + 48 * HALF) + 1 * 2**20

        def run(moments, plan):
            x2, y2, stats = pl.pallas_call(
                functools.partial(move_kernel, slots, cols),
                out_shape=(arrived, arrived, jax.ShapeDtypeStruct((8, blocks), f32)),
                in_specs=[hbm, hbm],
                out_specs=(vmem, vmem, vmem),
                scratch_shapes=[
                    pltpu.VMEM((blocks, sub, width), f32), pltpu.VMEM((blocks, sub, width), f32),
                    sent, sent, got, got, got, got, out, out,
                    pltpu.VMEM((4, blocks, 128), f32), stat, stat, stat,
                    pltpu.VMEM((peers, 8, blocks), f32),
                    pltpu.VMEM((SIDE - 1, 8, blocks), f32),
                    pltpu.VMEM((SIDE - 1, 8, blocks), f32),
                    pltpu.SMEM((128,), i32), dma, dma((2,)), dma((2, 2, 3)), dma((2, 2, 3)), dma((2, 2, 3)), dma((2, 2, 3)),
                    dma((peers,)), dma((peers,)), dma((2, 3)), dma((2, 3)),
                ],
                compiler_params=pltpu.CompilerParams(
                    collective_id=number, has_side_effects=True, vmem_limit_bytes=limit),
                name=f"move{slots}",
            )(plan, moments)
            return pl.pallas_call(
                functools.partial(place_kernel, float(sub * groups * width * cols)),
                out_shape=(
                    jax.ShapeDtypeStruct((tensors, capacity * sub * groups, width), f32),
                    jax.ShapeDtypeStruct((tensors, capacity), f32),
                    jax.ShapeDtypeStruct((tensors, capacity), f32),
                ),
                in_specs=[smem, vmem, vmem, vmem],
                out_specs=(hbm, hbm, hbm),
                scratch_shapes=[
                    pltpu.VMEM((tensors, capacity, sub * groups, width), f32),
                    pltpu.VMEM((sub * groups, width), f32),
                    pltpu.VMEM((tensors, capacity, 128), f32),
                    pltpu.VMEM((tensors, capacity), f32), pltpu.VMEM((tensors, capacity), f32),
                    dma((tensors, capacity)), dma((2,)),
                ],
                compiler_params=pltpu.CompilerParams(vmem_limit_bytes=16 * 2**20),
                name="place",
            )(plan, stats, x2, y2)

        return run

    return lax.switch(tier[0], [branch(i, s) for i, s in enumerate(TIERS)], moments, plan)


def solution(mesh):
    placed = (P(None, None, "row", "col"), P())
    return jax.shard_map(
        on_device,
        mesh=mesh,
        in_specs=placed,
        out_specs=(P(None, "row", "col"), P(None, "row"), P(None, "row")),
        check_vma=False,
    )
```

profile of v0, /device:TPU:1, one launch (start us, length us, event | category | flops | bytes accessed | tf_op | source)
XLA Modules:
  0.0 122.1 jit_solution(738605209632977584)
XLA Ops:
  0.6 1.6 %plan.1 = (s32[128]{0:T(128)S(1)}, s32[1]{0:T(128)}) custom-call(s32[16]{0:T(128)} %count_ref.1), custom_call_target="tpu_custom_call" | custom-call | tf_op jit(solution)/shard_map/plan/pallas_call | solution.py:307
  2.9 119.1 %conditional.1 = ((f32[2,2048,768]{2,1,0:T(8,128)}, f32[2,16]{1,0:T(2,128)}, f32[2,16]{1,0:T(2,128)})) conditional(s32[]{:T(128)} %bitcast, (s32[128]{0:T(128)S(1)}, f32[2,128,8,768]{3,2,1,0:T(8,128)}) %tuple.40, (s32[128]{0:T(128)S(1)}, f32[2,128,8,768]{3,2,1,0:T(8,128)}) %tuple.40, (s32[128]{0:T(128)S(1)}, ...), branch_computations={%region_0.0_spmd, %region_1.0_spmd, %region_2.0_spmd, %region_3.0_... | conditional | bytes 8 | solution.py:368
  2.9 113.4 %move17.1 = (f32[4,2,8,4,8,768]{5,4,3,2,1,0:T(8,128)S(1)}, f32[4,2,8,4,8,768]{5,4,3,2,1,0:T(8,128)S(1)}, f32[8,128]{1,0:T(8,128)S(1)}) custom-call(s32[128]{0:T(128)S(1)} %get-tuple-element.44.plan_in.plan_ref, f32[2,128,8,768]{3,2,1,0:T(8,128)} %get-tuple-element.45.moments_ref), custom_call_target="tpu_custom_call" | custom-call | tf_op jit(solution)/shard_map/cond/branch_0_fun/move17/pallas_call | solution.py:327
  116.3 5.4 %place.11 = (f32[2,2048,768]{2,1,0:T(8,128)}, f32[2,16]{1,0:T(2,128)}, f32[2,16]{1,0:T(2,128)}) custom-call(s32[128]{0:T(128)S(1)} %get-tuple-element.44.plan_in.plan_ref, f32[8,128]{1,0:T(8,128)S(1)} %get-tuple-element.46.stats_ref, f32[4,2,8,4,8,768]{5,4,3,2,1,0:T(8,128)S(1)} %get-tuple-element.47.x2_ref, f32[4,2,8,4,8,768]{5,4,3,2,1,0:T(8,128)S(1)} %get-tuple-element.48.y2_ref), custom_call_target="tpu_custom_call" | custom-call | tf_op jit(solution)/shard_map/cond/branch_0_fun/place/pallas_call | solution.py:346
where the time goes:
time: 123 us; the launch traced here: 122 us
  Pallas kernels  120 us (98%)
  between operations  1.47 us (1%)
    pallas_call x1, Pallas kernels, run(): pl.pallas_call(functools.partial(move_kernel, slots, cols), out_shape=(ar...  113 us
    pallas_call x1, Pallas kernels, run(): pl.pallas_call(functools.partial(place_kernel, float(sub * groups * width...  5.42 us

commit v1 on v0

--- a/solution.py
+++ b/solution.py
@@ -52,7 +52,7 @@
     slots, cols, plan_in, moments_ref, x2_ref, y2_ref, stats_ref,
     mom0, mom1, send_x, send_y, got_x0, got_x1, got_y0, got_y1, out_x, out_y,
     pieces, stat_a, stat_b, stat_c, all_a, all_b, all_c,
-    plan_ref, plan_sem, load_sem, send1, recv1, send2, recv2, sa, ra, sb, rb,
+    plan_ref, go_sem, plan_sem, load_sem, send1, recv1, send2, recv2, sa, ra, sb, rb,
 ):
     mom = (mom0, mom1)
     got_x = (got_x0, got_x1)
@@ -78,12 +78,16 @@
     def y_peer(d):
         return {"row": ((y + d) % SIDE) * SIDE + x}
 
+    core, z, planes = c % 2, c // 2, cols // 2
+    mate = {"col": z * 2 + 1 - core}
     barrier = pltpu.get_barrier_semaphore()
     for d in TURNS:
-        pl.semaphore_signal(barrier, inc=1, device_id=x_peer(d), device_id_type=MESH)
-        pl.semaphore_signal(barrier, inc=1, device_id=y_peer(d), device_id_type=MESH)
-    for d in range(1, cols):
-        pl.semaphore_signal(barrier, inc=1, device_id={"col": (c + d) % cols}, device_id_type=MESH)
+        pl.semaphore_signal(barrier, inc=1, device_id={**x_peer(d), "col": z * 2}, device_id_type=MESH)
+        pl.semaphore_signal(barrier, inc=1, device_id={**y_peer(d), "col": z * 2}, device_id_type=MESH)
+    for d in range(1, planes):
+        pl.semaphore_signal(
+            barrier, inc=1, device_id={"col": ((z + d) % planes) * 2 + 1}, device_id_type=MESH)
+    pl.semaphore_signal(barrier, inc=1, device_id=mate, device_id_type=MESH)
 
     def order_x(xd):
         at = [plan_ref[2 * GROUPS + i * SIDE + xd] for i in range(SIDE)]
@@ -120,7 +124,15 @@
         lax.fori_loop(0, slots, step, 0, unroll=2)
 
     table.wait()
-    pl.semaphore_wait(barrier, 2 * (SIDE - 1) + cols - 1)
+
+    @pl.when(core == 0)
+    def _():
+        pl.semaphore_wait(barrier, 4 * (SIDE - 1) + 1)
+        pl.semaphore_signal(go_sem, inc=1, device_id=mate, device_id_type=MESH)
+
+    @pl.when(core == 1)
+    def _():
+        pl.semaphore_wait(go_sem, 1)
 
     first = [[], []]
     for t in range(tensors):
@@ -167,6 +179,16 @@
             o = others[i]
             v = jnp.where(is_peak, jnp.maximum(v, o), v + o)
         return v
+
+
+    @pl.when(core == 1)
+    def _():
+        pl.semaphore_wait(barrier, 2 * planes - 1)
+        pl.semaphore_signal(go_sem, inc=1, device_id=mate, device_id_type=MESH)
+
+    @pl.when(core == 0)
+    def _():
+        pl.semaphore_wait(go_sem, 1)
 
     stage = []
     for d in range(1, cols):
@@ -336,7 +358,7 @@
                     pltpu.VMEM((peers, 8, blocks), f32),
                     pltpu.VMEM((SIDE - 1, 8, blocks), f32),
                     pltpu.VMEM((SIDE - 1, 8, blocks), f32),
-                    pltpu.SMEM((128,), i32), dma, dma((2,)), dma((2, 2, 3)), dma((2, 2, 3)), dma((2, 2, 3)), dma((2, 2, 3)),
+                    pltpu.SMEM((128,), i32), pltpu.SemaphoreType.REGULAR, dma, dma((2,)), dma((2, 2, 3)), dma((2, 2, 3)), dma((2, 2, 3)), dma((2, 2, 3)),
                     dma((peers,)), dma((peers,)), dma((2, 3)), dma((2, 3)),
                 ],
                 compiler_params=pltpu.CompilerParams(

time: 123 us -> 137 us (1.11)
  Pallas kernels: 120 us -> 135 us
    pallas_call x1, Pallas kernels: 113 us -> 128 us  [run(): pl.pallas_call(functools.partial(move_kernel, slots, cols), out_shape=(ar...]
where the time goes in v1:
time: 137 us
  Pallas kernels  135 us (99%)
  between operations  1.47 us (1%)
    pallas_call x1, Pallas kernels, run(): pl.pallas_call(functools.partial(move_kernel, slots, cols), out_shape=(ar...  128 us
    pallas_call x1, Pallas kernels, run(): pl.pallas_call(functools.partial(place_kernel, float(sub * groups * width...  5.42 us

profile of v1, /device:TPU:1, one launch (start us, length us, event | category | flops | bytes accessed | tf_op | source)
XLA Modules:
  0.0 136.9 jit_solution(10549397098959539572)
XLA Ops:
  0.6 1.6 %plan.1 = (s32[128]{0:T(128)S(1)}, s32[1]{0:T(128)}) custom-call(s32[16]{0:T(128)} %count_ref.1), custom_call_target="tpu_custom_call" | custom-call | tf_op jit(solution)/shard_map/plan/pallas_call | solution.py:329
  2.9 133.8 %conditional.1 = ((f32[2,2048,768]{2,1,0:T(8,128)}, f32[2,16]{1,0:T(2,128)}, f32[2,16]{1,0:T(2,128)})) conditional(s32[]{:T(128)} %bitcast, (s32[128]{0:T(128)S(1)}, f32[2,128,8,768]{3,2,1,0:T(8,128)}) %tuple.40, (s32[128]{0:T(128)S(1)}, f32[2,128,8,768]{3,2,1,0:T(8,128)}) %tuple.40, (s32[128]{0:T(128)S(1)}, ...), branch_computations={%region_0.0_spmd, %region_1.0_spmd, %region_2.0_spmd, %region_3.0_... | conditional | bytes 8 | solution.py:390
  2.9 128.0 %move24.1 = (f32[4,2,8,4,8,768]{5,4,3,2,1,0:T(8,128)S(1)}, f32[4,2,8,4,8,768]{5,4,3,2,1,0:T(8,128)S(1)}, f32[8,128]{1,0:T(8,128)S(1)}) custom-call(s32[128]{0:T(128)S(1)} %get-tuple-element.79.plan_in.plan_ref, f32[2,128,8,768]{3,2,1,0:T(8,128)} %get-tuple-element.80.moments_ref), custom_call_target="tpu_custom_call" | custom-call | tf_op jit(solution)/shard_map/cond/branch_7_fun/move24/pallas_call | solution.py:349
  130.9 5.4 %place.18 = (f32[2,2048,768]{2,1,0:T(8,128)}, f32[2,16]{1,0:T(2,128)}, f32[2,16]{1,0:T(2,128)}) custom-call(s32[128]{0:T(128)S(1)} %get-tuple-element.79.plan_in.plan_ref, f32[8,128]{1,0:T(8,128)S(1)} %get-tuple-element.81.stats_ref, f32[4,2,8,4,8,768]{5,4,3,2,1,0:T(8,128)S(1)} %get-tuple-element.82.x2_ref, f32[4,2,8,4,8,768]{5,4,3,2,1,0:T(8,128)S(1)} %get-tuple-element.83.y2_ref), custom_call_target="tpu_custom_call" | custom-call | tf_op jit(solution)/shard_map/cond/branch_7_fun/place/pallas_call | solution.py:368

commit v2 on v1

--- a/solution.py
+++ b/solution.py
@@ -49,10 +49,10 @@
 
 
 def move_kernel(
-    slots, cols, plan_in, moments_ref, x2_ref, y2_ref, stats_ref,
+    slots, cols, plan_ref, moments_ref, x2_ref, y2_ref, stats_ref,
     mom0, mom1, send_x, send_y, got_x0, got_x1, got_y0, got_y1, out_x, out_y,
     pieces, stat_a, stat_b, stat_c, all_a, all_b, all_c,
-    plan_ref, go_sem, plan_sem, load_sem, send1, recv1, send2, recv2, sa, ra, sb, rb,
+    go_sem, load_sem, send1, recv1, send2, recv2, sa, ra, sb, rb,
 ):
     mom = (mom0, mom1)
     got_x = (got_x0, got_x1)
@@ -67,8 +67,6 @@
         pltpu.make_async_copy(moments_ref.at[t], mom[t], load_sem.at[t])
         for t in range(tensors)
     ]
-    table = pltpu.make_async_copy(plan_in, plan_ref, plan_sem)
-    table.start()
     for load in loads:
         load.start()
 
@@ -123,7 +121,6 @@
 
         lax.fori_loop(0, slots, step, 0, unroll=2)
 
-    table.wait()
 
     @pl.when(core == 0)
     def _():
@@ -328,7 +325,7 @@
 
     plan, tier = pl.pallas_call(
         plan_kernel,
-        out_shape=(jax.ShapeDtypeStruct((128,), i32), jax.ShapeDtypeStruct((1,), i32)),
+        out_shape=(pltpu.SMEM((128,), i32), pltpu.SMEM((1,), i32)),
         in_specs=[smem],
         out_specs=(smem, smem),
         name="plan",
@@ -349,7 +346,7 @@
             x2, y2, stats = pl.pallas_call(
                 functools.partial(move_kernel, slots, cols),
                 out_shape=(arrived, arrived, jax.ShapeDtypeStruct((8, blocks), f32)),
-                in_specs=[hbm, hbm],
+                in_specs=[smem, hbm],
                 out_specs=(vmem, vmem, vmem),
                 scratch_shapes=[
                     pltpu.VMEM((blocks, sub, width), f32), pltpu.VMEM((blocks, sub, width), f32),
@@ -358,7 +355,7 @@
                     pltpu.VMEM((peers, 8, blocks), f32),
                     pltpu.VMEM((SIDE - 1, 8, blocks), f32),
                     pltpu.VMEM((SIDE - 1, 8, blocks), f32),
-                    pltpu.SMEM((128,), i32), pltpu.SemaphoreType.REGULAR, dma, dma((2,)), dma((2, 2, 3)), dma((2, 2, 3)), dma((2, 2, 3)), dma((2, 2, 3)),
+                    pltpu.SemaphoreType.REGULAR, dma((2,)), dma((2, 2, 3)), dma((2, 2, 3)), dma((2, 2, 3)), dma((2, 2, 3)),
                     dma((peers,)), dma((peers,)), dma((2, 3)), dma((2, 3)),
                 ],
                 compiler_params=pltpu.CompilerParams(

time: 137 us -> 120 us (0.88)
  Pallas kernels: 135 us -> 119 us
    pallas_call x1, Pallas kernels: 128 us -> 113 us  [run(): pl.pallas_call(functools.partial(move_kernel, slots, cols), out_shape=(ar...]
where the time goes in v2:
time: 120 us
  Pallas kernels  119 us (99%)
    pallas_call x1, Pallas kernels, run(): pl.pallas_call(functools.partial(move_kernel, slots, cols), out_shape=(ar...  113 us
    pallas_call x1, Pallas kernels, run(): pl.pallas_call(functools.partial(place_kernel, float(sub * groups * width...  4.9 us

profile of v2, /device:TPU:1, one launch (start us, length us, event | category | flops | bytes accessed | tf_op | source)
XLA Modules:
  0.0 120.1 jit_solution(7891046757084430282)
XLA Ops:
  0.6 1.0 plan.1
  1.7 118.3 %conditional.1 = ((f32[2,2048,768]{2,1,0:T(8,128)}, f32[2,16]{1,0:T(2,128)}, f32[2,16]{1,0:T(2,128)})) conditional(s32[]{:T(128)} %bitcast, (s32[128]{0:T(128)S(4)}, f32[2,128,8,768]{3,2,1,0:T(8,128)}) %tuple.40, (s32[128]{0:T(128)S(4)}, f32[2,128,8,768]{3,2,1,0:T(8,128)}) %tuple.40, (s32[128]{0:T(128)S(4)}, ...), branch_computations={%region_0.0_spmd, %region_1.0_spmd, %region_2.0_spmd, %region_3.0_... | conditional | bytes 8 | solution.py:387
  1.7 113.1 %move17.1 = (f32[4,2,8,4,8,768]{5,4,3,2,1,0:T(8,128)S(1)}, f32[4,2,8,4,8,768]{5,4,3,2,1,0:T(8,128)S(1)}, f32[8,128]{1,0:T(8,128)S(1)}) custom-call(s32[128]{0:T(128)S(4)} %get-tuple-element.44.plan_ref, f32[2,128,8,768]{3,2,1,0:T(8,128)} %get-tuple-element.45.moments_ref), custom_call_target="tpu_custom_call" | custom-call | tf_op jit(solution)/shard_map/cond/branch_0_fun/move17/pallas_call | solution.py:346
  114.8 4.9 %place.11 = (f32[2,2048,768]{2,1,0:T(8,128)}, f32[2,16]{1,0:T(2,128)}, f32[2,16]{1,0:T(2,128)}) custom-call(s32[128]{0:T(128)S(4)} %get-tuple-element.44.plan_ref, f32[8,128]{1,0:T(8,128)S(1)} %get-tuple-element.46.stats_ref, f32[4,2,8,4,8,768]{5,4,3,2,1,0:T(8,128)S(1)} %get-tuple-element.47.x2_ref, f32[4,2,8,4,8,768]{5,4,3,2,1,0:T(8,128)S(1)} %get-tuple-element.48.y2_ref), custom_call_target="tpu_custom_call" | custom-call | tf_op jit(solution)/shard_map/cond/branch_0_fun/place/pallas_call | solution.py:365

commit v3 on v2

--- a/solution.py
+++ b/solution.py
@@ -9,7 +9,7 @@
 SIDE = 4
 GROUPS = SIDE * SIDE
 HALF = 8
-TIERS = (17, 18, 19, 20, 21, 22, 23, 24, 26, 28, 32)
+TIERS = (16, 17, 18, 19, 20, 21, 22, 24, 25, 28, 32)
 MESH = pl.DeviceIdType.MESH
 TURNS = (1, 3, 2)
 
@@ -22,7 +22,7 @@
     a = [(n[g] + (g // SIDE + g % SIDE) % 2) // 2 for g in range(groups)]
     col = [sum(a[x::SIDE]) for x in range(SIDE)]
     row = [sum(n[y * SIDE:(y + 1) * SIDE]) - sum(a[y * SIDE:(y + 1) * SIDE]) for y in range(SIDE)]
-    for _ in range(2):
+    for _ in range(3):
         for g in range(groups):
             y, x = divmod(g, SIDE)
             new = jnp.clip(a[g] - ((col[x] - row[y] + 1) >> 1), low[g], high[g])
@@ -80,8 +80,9 @@
     mate = {"col": z * 2 + 1 - core}
     barrier = pltpu.get_barrier_semaphore()
     for d in TURNS:
-        pl.semaphore_signal(barrier, inc=1, device_id={**x_peer(d), "col": z * 2}, device_id_type=MESH)
-        pl.semaphore_signal(barrier, inc=1, device_id={**y_peer(d), "col": z * 2}, device_id_type=MESH)
+        side = z * 2 + (1 if d == 2 else 0)
+        pl.semaphore_signal(barrier, inc=1, device_id={**x_peer(d), "col": side}, device_id_type=MESH)
+        pl.semaphore_signal(barrier, inc=1, device_id={**y_peer(d), "col": side}, device_id_type=MESH)
     for d in range(1, planes):
         pl.semaphore_signal(
             barrier, inc=1, device_id={"col": ((z + d) % planes) * 2 + 1}, device_id_type=MESH)
@@ -124,7 +125,7 @@
 
     @pl.when(core == 0)
     def _():
-        pl.semaphore_wait(barrier, 4 * (SIDE - 1) + 1)
+        pl.semaphore_wait(barrier, 9)
         pl.semaphore_signal(go_sem, inc=1, device_id=mate, device_id_type=MESH)
 
     @pl.when(core == 1)
@@ -132,21 +133,38 @@
         pl.semaphore_wait(go_sem, 1)
 
     first = [[], []]
+
+    def send1_to(t, i, d):
+        pack1(t, order_x((x + d) % SIDE), send_x.at[t, i])
+        copy = pltpu.make_async_remote_copy(
+            send_x.at[t, i], got_x[t].at[x], send1.at[t, 0, i], recv1.at[t, 0, i],
+            device_id=x_peer(d), device_id_type=MESH)
+        copy.start()
+        first[t].append(copy)
+        pack1(t, order_y((y + d) % SIDE), send_y.at[t, i])
+        copy = pltpu.make_async_remote_copy(
+            send_y.at[t, i], got_y[t].at[y], send1.at[t, 1, i], recv1.at[t, 1, i],
+            device_id=y_peer(d), device_id_type=MESH)
+        copy.start()
+        first[t].append(copy)
+
     for t in range(tensors):
         loads[t].wait()
-        for i, d in enumerate(TURNS):
-            pack1(t, order_x((x + d) % SIDE), send_x.at[t, i])
-            copy = pltpu.make_async_remote_copy(
-                send_x.at[t, i], got_x[t].at[x], send1.at[t, 0, i], recv1.at[t, 0, i],
-                device_id=x_peer(d), device_id_type=MESH)
-            copy.start()
-            first[t].append(copy)
-            pack1(t, order_y((y + d) % SIDE), send_y.at[t, i])
-            copy = pltpu.make_async_remote_copy(
-                send_y.at[t, i], got_y[t].at[y], send1.at[t, 1, i], recv1.at[t, 1, i],
-                device_id=y_peer(d), device_id_type=MESH)
-            copy.start()
-            first[t].append(copy)
+        for i, d in enumerate(TURNS[:2]):
+            send1_to(t, i, d)
+
+    @pl.when(core == 1)
+    def _():
+        pl.semaphore_wait(barrier, 2 * planes + 3)
+        pl.semaphore_signal(go_sem, inc=1, device_id=mate, device_id_type=MESH)
+
+    @pl.when(core == 0)
+    def _():
+        pl.semaphore_wait(go_sem, 1)
+
+    for t in range(tensors):
+        send1_to(t, 2, TURNS[2])
+    for t in range(tensors):
         pack1(t, order_x(x), got_x[t].at[x])
         pack1(t, order_y(y), got_y[t].at[y])
 
@@ -177,15 +195,6 @@
             v = jnp.where(is_peak, jnp.maximum(v, o), v + o)
         return v
 
-
-    @pl.when(core == 1)
-    def _():
-        pl.semaphore_wait(barrier, 2 * planes - 1)
-        pl.semaphore_signal(go_sem, inc=1, device_id=mate, device_id_type=MESH)
-
-    @pl.when(core == 0)
-    def _():
-        pl.semaphore_wait(go_sem, 1)
 
     stage = []
     for d in range(1, cols):

time: 120 us -> 120 us (level); the launches traced: 120 us -> 118 us
  Pallas kernels: 119 us -> 117 us
    pallas_call x1, Pallas kernels: 113 us -> 111 us  [run(): pl.pallas_call(functools.partial(move_kernel, slots, cols), out_shape=(ar...]
where the time goes in v3:
time: 120 us; the launch traced here: 118 us
  Pallas kernels  117 us (98%)
    pallas_call x1, Pallas kernels, run(): pl.pallas_call(functools.partial(move_kernel, slots, cols), out_shape=(ar...  111 us
    pallas_call x1, Pallas kernels, run(): pl.pallas_call(functools.partial(place_kernel, float(sub * groups * width...  4.88 us

profile of v3, /device:TPU:1, one launch (start us, length us, event | category | flops | bytes accessed | tf_op | source)
XLA Modules:
  0.0 117.7 jit_solution(15923075750380863370)
XLA Ops:
  0.6 1.1 plan.1
  1.7 115.8 %conditional.1 = ((f32[2,2048,768]{2,1,0:T(8,128)}, f32[2,16]{1,0:T(2,128)}, f32[2,16]{1,0:T(2,128)})) conditional(s32[]{:T(128)} %bitcast, (s32[128]{0:T(128)S(4)}, f32[2,128,8,768]{3,2,1,0:T(8,128)}) %tuple.40, (s32[128]{0:T(128)S(4)}, f32[2,128,8,768]{3,2,1,0:T(8,128)}) %tuple.40, (s32[128]{0:T(128)S(4)}, ...), branch_computations={%region_0.0_spmd, %region_1.0_spmd, %region_2.0_spmd, %region_3.0_... | conditional | bytes 8 | solution.py:396
  1.8 110.6 %move16.1 = (f32[4,2,8,4,8,768]{5,4,3,2,1,0:T(8,128)S(1)}, f32[4,2,8,4,8,768]{5,4,3,2,1,0:T(8,128)S(1)}, f32[8,128]{1,0:T(8,128)S(1)}) custom-call(s32[128]{0:T(128)S(4)} %get-tuple-element.44.plan_ref, f32[2,128,8,768]{3,2,1,0:T(8,128)} %get-tuple-element.45.moments_ref), custom_call_target="tpu_custom_call" | custom-call | tf_op jit(solution)/shard_map/cond/branch_0_fun/move16/pallas_call | solution.py:355
  112.4 4.9 %place.11 = (f32[2,2048,768]{2,1,0:T(8,128)}, f32[2,16]{1,0:T(2,128)}, f32[2,16]{1,0:T(2,128)}) custom-call(s32[128]{0:T(128)S(4)} %get-tuple-element.44.plan_ref, f32[8,128]{1,0:T(8,128)S(1)} %get-tuple-element.46.stats_ref, f32[4,2,8,4,8,768]{5,4,3,2,1,0:T(8,128)S(1)} %get-tuple-element.47.x2_ref, f32[4,2,8,4,8,768]{5,4,3,2,1,0:T(8,128)S(1)} %get-tuple-element.48.y2_ref), custom_call_target="tpu_custom_call" | custom-call | tf_op jit(solution)/shard_map/cond/branch_0_fun/place/pallas_call | solution.py:374
